TPU v7x, 32 devices: a whole 2x2x4 slice. The times are simulated.
32 devices in a mesh: groups: 2 (over x), tile: 16 (over z, y, core).
Axes of the slice: x: 2, y: 2, z: 4, core: 2. Of those that a mesh axis runs over, the one named last changes fastest.
Arguments:
- self_query: bfloat16 [4096, 4096], P(('groups', 'tile')), parts along dimension 0, may hold values from -110 to 110
- self_key: bfloat16 [4096, 4096], P(('groups', 'tile')), parts along dimension 0, may hold values from -6 to 6
- self_value: bfloat16 [4096, 4096], P(('groups', 'tile')), parts along dimension 0, may hold values from -24 to 24
- cross_query: bfloat16 [4096, 4096], P(('groups', 'tile')), parts along dimension 0, may hold values from -110 to 110
- text_key: bfloat16 [512, 4096], P(('groups', 'tile')), parts along dimension 0, may hold values from -6 to 6
- text_value: bfloat16 [512, 4096], P(('groups', 'tile')), parts along dimension 0, may hold values from -24 to 24
- timestep: int32 [1], replicated, may hold values from 0 to 49
- gate_table: bfloat16 [50, 4096], replicated, may hold values from 0.5 to 2
Outputs:
- mixed: bfloat16 [4096, 4096], P(('groups', 'tile')), parts along dimension 0
There are 2 independent parts, one for each index of `groups`. A program takes and returns all parts, laid end to end along the dimension named above; an argument that names none is the same for every part. Nothing has to cross between parts.
All inputs are finite; a program needn't handle non-finite values.
Results may differ from a plain program's by a relative error of at most 0.0032.
Values may be sent and summed in bfloat16 or wider, within the bound.
A program may use at most 64 MiB of HBM per device.

v0:
```python
import math

import jax
import jax.numpy as jnp
from jax import lax
from jax.sharding import PartitionSpec as P

HEADS = 32
RADIUS = 2


def from_behind(block, axis, distance):
    devices = range(lax.axis_size(axis))
    route = [(i - distance, i) for i in devices if i - distance in devices]
    return lax.ppermute(block, axis, route)


def attend_blocks(queries, key_stack, value_stack, tile_usable):
    row_count, width = queries.shape
    window_span, key_count = (key_stack.shape[0], key_stack.shape[1])
    head_dim = width // HEADS
    head_group = math.gcd(HEADS, 8)
    score_scale = 1.0 / math.sqrt(head_dim)
    usable = tile_usable[None, None, :, None]
    pieces = []
    for block_index in range(HEADS // head_group):
        first = block_index * head_group * head_dim
        last = first + head_group * head_dim
        query_part = queries[:, first:last].reshape(row_count, head_group, head_dim)
        key_part = key_stack[:, :, first:last].reshape(window_span, key_count, head_group, head_dim)
        value_part = value_stack[:, :, first:last].reshape(
            window_span, key_count, head_group, head_dim
        )
        scores = (
            jnp.einsum("qhd,wkhd->hqwk", query_part, key_part, preferred_element_type=jnp.float32)
            * score_scale
        )
        masked = jnp.where(usable, scores, -1e30)
        maxima = jnp.max(masked, axis=(2, 3), keepdims=True)
        weights = jnp.where(usable, jnp.exp(masked - maxima), 0.0)
        totals = jnp.sum(weights, axis=(2, 3))
        rounded = weights.astype(jnp.bfloat16)
        summed = jnp.einsum(
            "hqwk,wkhd->qhd", rounded, value_part, preferred_element_type=jnp.float32
        )
        result = summed / jnp.transpose(totals)[:, :, None]
        pieces.append(result.reshape(row_count, head_group * head_dim))
    return jnp.concatenate(pieces, axis=1)


def shards(
    self_query, self_key, self_value, cross_query, text_key, text_value, timestep, gate_table
):
    radius = RADIUS
    tile_count = lax.axis_size("tile")
    tile_place = lax.axis_index("tile")
    text_keys, text_values = (
        lax.all_gather(text_key, "tile", axis=0, tiled=True),
        lax.all_gather(text_value, "tile", axis=0, tiled=True),
    )
    text_usable = jnp.ones((1,), dtype=bool)
    cross_out = attend_blocks(cross_query, text_keys[None], text_values[None], text_usable)
    own_pair = (self_key, self_value)
    received = {0: own_pair}
    above_pair = own_pair
    below_pair = own_pair
    for distance in range(1, radius + 1):
        above_pair = from_behind((above_pair[0], above_pair[1]), "tile", -1)
        below_pair = from_behind((below_pair[0], below_pair[1]), "tile", 1)
        received[distance] = above_pair
        received[-distance] = below_pair
    ordered = [received[offset] for offset in range(-radius, radius + 1)]
    key_stack = jnp.stack([pair[0] for pair in ordered])
    value_stack = jnp.stack([pair[1] for pair in ordered])
    offsets = jnp.arange(2 * radius + 1, dtype=jnp.int32) - radius
    position = tile_place + offsets
    tile_usable = (position >= 0) & (position < tile_count)
    self_out = attend_blocks(self_query, key_stack, value_stack, tile_usable)
    gate_row = lax.dynamic_slice_in_dim(gate_table, timestep[0], 1, 0).astype(jnp.float32)
    return (gate_row * self_out + cross_out).astype(jnp.bfloat16)


def solution(mesh):
    in_specs = (
        P(("groups", "tile"), None),
        P(("groups", "tile"), None),
        P(("groups", "tile"), None),
        P(("groups", "tile"), None),
        P(("groups", "tile"), None),
        P(("groups", "tile"), None),
        P(),
        P(),
    )
    out_specs = P(("groups", "tile"), None)
    return jax.shard_map(shards, mesh=mesh, in_specs=in_specs, out_specs=out_specs, check_vma=False)
```

profile of v0, /device:TPU:17, one launch (start us, length us, event | category | flops | bytes accessed | tf_op | source)
XLA Modules:
  0.0 183.5 jit_solution(7587704553490740016)
XLA Ops:
  7.3 1.6 copy.76
  8.9 3.7 %collective-permute-start = (bf16[128,4096]{0,1:T(8,128)(2,1)S(1)}, bf16[128,4096]{0,1:T(8,128)(2,1)}, u32[]{:S(2)}, u32[]{:S(2)}) collective-permute-start(bf16[128,4096]{0,1:T(8,128)(2,1)S(1)} %copy.76), channel_id=1, source_target_pairs={{0,1},{1,2},{2,3},{3,4},{4,5},{5,6},{6,7},{7,8},{8,9},{9,10},{10,1... | collective-permute-start | bytes 3145736 | tf_op jit(solution)/shard_map/ppermute | solution.py:15
  12.6 1.9 %collective-permute-start.2 = (bf16[128,4096]{0,1:T(8,128)(2,1)S(1)}, bf16[128,4096]{0,1:T(8,128)(2,1)}, u32[]{:S(2)}, u32[]{:S(2)}) collective-permute-start(bf16[128,4096]{0,1:T(8,128)(2,1)S(1)} %copy.76), channel_id=1, source_target_pairs={{1,0},{2,1},{3,2},{4,3},{5,4},{6,5},{7,6},{8,7},{9,8},{10,9},{11,1... | collective-permute-start | bytes 3145736 | tf_op jit(solution)/shard_map/ppermute | solution.py:15
  15.3 3.6 %collective-permute-start.4 = (bf16[128,4096]{0,1:T(8,128)(2,1)S(1)}, bf16[128,4096]{0,1:T(8,128)(2,1)}, u32[]{:S(2)}, u32[]{:S(2)}) collective-permute-start(bf16[128,4096]{0,1:T(8,128)(2,1)S(1)} %copy.79), channel_id=1, source_target_pairs={{0,1},{1,2},{2,3},{3,4},{4,5},{5,6},{6,7},{7,8},{8,9},{9,10},{10,1... | collective-permute-start | bytes 3145736 | tf_op jit(solution)/shard_map/ppermute | solution.py:15
  18.9 1.9 %collective-permute-start.6 = (bf16[128,4096]{0,1:T(8,128)(2,1)S(1)}, bf16[128,4096]{0,1:T(8,128)(2,1)}, u32[]{:S(2)}, u32[]{:S(2)}) collective-permute-start(bf16[128,4096]{0,1:T(8,128)(2,1)S(1)} %copy.79), channel_id=1, source_target_pairs={{1,0},{2,1},{3,2},{4,3},{5,4},{6,5},{7,6},{8,7},{9,8},{10,9},{11,1... | collective-permute-start | bytes 3145736 | tf_op jit(solution)/shard_map/ppermute | solution.py:15
  20.9 44.2 %collective-permute-done = bf16[128,4096]{0,1:T(8,128)(2,1)} collective-permute-done((bf16[128,4096]{0,1:T(8,128)(2,1)S(1)}, bf16[128,4096]{0,1:T(8,128)(2,1)}, u32[]{:S(2)}, u32[]{:S(2)}) %collective-permute-start) | collective-permute-done | bytes 1048608 | tf_op jit(solution)/shard_map/ppermute | solution.py:15
  65.1 4.5 %collective-permute-start.1 = (bf16[128,4096]{0,1:T(8,128)(2,1)}, bf16[128,4096]{0,1:T(8,128)(2,1)}, u32[]{:S(2)}, u32[]{:S(2)}) collective-permute-start(bf16[128,4096]{0,1:T(8,128)(2,1)} %collective-permute-done), channel_id=1, source_target_pairs={{0,1},{1,2},{2,3},{3,4},{4,5},{5,6},{6,7},{7,8},{8,9},{9,10},{10,1... | collective-permute-start | bytes 3145736 | tf_op jit(solution)/shard_map/ppermute | solution.py:15
  72.9 2.0 %fusion.82 = (bf16[128,1024]{1,0:T(8,128)(2,1)S(1)}, bf16[128,1024]{1,0:T(8,128)(2,1)S(1)}, bf16[128,1024]{1,0:T(8,128)(2,1)S(1)}, bf16[128,1024]{1,0:T(8,128)(2,1)}) fusion(bf16[128,4096]{1,0:T(8,128)(2,1)} %param.11), kind=kLoop, calls=%fused_computation.99 | loop fusion | bytes 2097152 | tf_op jit(solution)/shard_map/slice | solution.py:29
  74.9 1.8 copy.166
  80.1 1.9 %collective-permute-start.3 = (bf16[128,4096]{0,1:T(8,128)(2,1)}, bf16[128,4096]{0,1:T(8,128)(2,1)S(1)}, u32[]{:S(2)}, u32[]{:S(2)}) collective-permute-start(bf16[128,4096]{0,1:T(8,128)(2,1)} %collective-permute-done.2), channel_id=1, source_target_pairs={{1,0},{2,1},{3,2},{4,3},{5,4},{6,5},{7,6},{8,7},{9,8},{10,9},{11,1... | collective-permute-start | bytes 3145736 | tf_op jit(solution)/shard_map/ppermute | solution.py:15
  82.0 3.6 %collective-permute-start.5 = (bf16[128,4096]{0,1:T(8,128)(2,1)}, bf16[128,4096]{0,1:T(8,128)(2,1)S(1)}, u32[]{:S(2)}, u32[]{:S(2)}) collective-permute-start(bf16[128,4096]{0,1:T(8,128)(2,1)} %collective-permute-done.4), channel_id=1, source_target_pairs={{0,1},{1,2},{2,3},{3,4},{4,5},{5,6},{6,7},{7,8},{8,9},{9,10},{10,1... | collective-permute-start | bytes 3145736 | tf_op jit(solution)/shard_map/ppermute | solution.py:15
  85.7 1.9 %collective-permute-start.7 = (bf16[128,4096]{0,1:T(8,128)(2,1)}, bf16[128,4096]{0,1:T(8,128)(2,1)S(1)}, u32[]{:S(2)}, u32[]{:S(2)}) collective-permute-start(bf16[128,4096]{0,1:T(8,128)(2,1)} %collective-permute-done.6), channel_id=1, source_target_pairs={{1,0},{2,1},{3,2},{4,3},{5,4},{6,5},{7,6},{8,7},{9,8},{10,9},{11,1... | collective-permute-start | bytes 3145736 | tf_op jit(solution)/shard_map/ppermute | solution.py:15
  87.6 2.8 %collective-permute-done.1 = bf16[128,4096]{0,1:T(8,128)(2,1)} collective-permute-done((bf16[128,4096]{0,1:T(8,128)(2,1)}, bf16[128,4096]{0,1:T(8,128)(2,1)}, u32[]{:S(2)}, u32[]{:S(2)}) %collective-permute-start.1) | collective-permute-done | bytes 1048608 | tf_op jit(solution)/shard_map/ppermute | solution.py:15
  90.4 1.3 bitcast_dynamic-update-slice_fusion.9
  91.7 1.4 bitcast_dynamic-update-slice_fusion.8
  93.2 24.0 %collective-permute-done.5 = bf16[128,4096]{0,1:T(8,128)(2,1)S(1)} collective-permute-done((bf16[128,4096]{0,1:T(8,128)(2,1)}, bf16[128,4096]{0,1:T(8,128)(2,1)S(1)}, u32[]{:S(2)}, u32[]{:S(2)}) %collective-permute-start.5) | collective-permute-done | bytes 1048608 | tf_op jit(solution)/shard_map/ppermute | solution.py:15
  117.2 1.4 bitcast_dynamic-update-slice_fusion.3
  118.7 1.4 bitcast_dynamic-update-slice_fusion.1
  120.1 4.4 %collective-permute-done.7 = bf16[128,4096]{0,1:T(8,128)(2,1)S(1)} collective-permute-done((bf16[128,4096]{0,1:T(8,128)(2,1)}, bf16[128,4096]{0,1:T(8,128)(2,1)S(1)}, u32[]{:S(2)}, u32[]{:S(2)}) %collective-permute-start.7) | collective-permute-done | bytes 1048608 | tf_op jit(solution)/shard_map/ppermute | solution.py:15
  125.1 1.4 bitcast_dynamic-update-slice_fusion.6
  127.8 1.8 %fusion.78 = (bf16[5,128,1024]{1,2,0:T(8,128)(2,1)S(1)}, bf16[5,128,1024]{1,2,0:T(8,128)(2,1)S(1)}, bf16[5,128,1024]{1,2,0:T(8,128)(2,1)}, bf16[5,128,1024]{1,2,0:T(8,128)(2,1)}) fusion(bf16[5,128,4096]{1,2,0:T(8,128)(2,1)S(1)} %bitcast_dynamic-update-slice_fusion.5), kind=kLoop, calls=%fused_computation.95 | loop fusion | bytes 10485760 | tf_op jit(solution)/shard_map/slice | solution.py:31
  130.7 4.0 %fusion.10 = (f32[8,128]{1,0:T(8,128)S(1)}, f32[8,128]{1,0:T(8,128)S(1)}, f32[8,128]{1,0:T(8,128)S(1)}, f32[8,128]{1,0:T(8,128)S(1)}, bf16[8,128,5,128]{1,3,2,0:...) fusion(f32[8,5,128,128]{3,2,1,0:T(8,128)S(1)} %get-tuple-element.41, ...), kind=kOutput, calls=%fused_computation.23 | convolution fusion | flops 179564544 | bytes 14704645 | tf_op jit(solution)/shard_map/qhd,wkhd->hqwk/dot_general | solution.py:35
  134.7 2.6 %fusion.14 = (f32[8,128]{1,0:T(8,128)S(1)}, f32[8,128]{1,0:T(8,128)S(1)}, bf16[8,128,5,128]{1,3,2,0:T(8,128)(2,1)}, bf16[8,128,5,128]{1,3,2,0:T(8,128)(2,1)S(1)}) fusion(f32[8,5,128,128]{3,2,1,0:T(8,128)S(1)} %get-tuple-element.42, f32[8,128]{1,0:T(8,128)S(1)} %get-tuple-element.6, pred[5]{0:T(512)(128)(4,1)S(1)} %compare_and_fusion, ...), kind=kLoop, calls=%fused_computation.27 | loop fusion | flops 7862272 | bytes 7880709 | tf_op jit(solution)/shard_map/reduce_sum | solution.py:41
  138.1 2.2 %fusion.53 = f32[128,8,128]{0,2,1:T(8,128)S(1)} fusion(bf16[5,128,8,128]{1,3,2,0:T(8,128)(2,1)} %bitcast.197, bf16[8,128,5,128]{1,3,2,0:T(8,128)(2,1)} %get-tuple-element.23, f32[128,8]{0,1:T(8,128)S(1)} %bitcast.222), kind=kOutput, calls=%fused_computation.78 | convolution fusion | flops 167903232 | bytes 3149824 | tf_op jit(solution)/shard_map/hqwk,wkhd->qhd/dot_general | solution.py:43
  140.5 2.2 %fusion.56 = f32[128,8,128]{0,2,1:T(8,128)S(1)} fusion(bf16[5,128,8,128]{1,3,2,0:T(8,128)(2,1)} %bitcast.196, bf16[8,128,5,128]{1,3,2,0:T(8,128)(2,1)} %get-tuple-element.22, f32[128,8]{0,1:T(8,128)S(1)} %bitcast.229), kind=kOutput, calls=%fused_computation.79 | convolution fusion | flops 167903232 | bytes 3149824 | tf_op jit(solution)/shard_map/hqwk,wkhd->qhd/dot_general | solution.py:43
  143.7 1.8 fusion.59
  146.5 2.7 %fusion.81 = (bf16[1,256,1024]{2,1,0:T(8,128)(2,1)}, bf16[1,256,1024]{2,1,0:T(8,128)(2,1)S(1)}, bf16[1,256,1024]{2,1,0:T(8,128)(2,1)}, bf16[1,256,1024]{2,1,0:T(8,128)(2,1)}) fusion(bf16[1,256,4096]{2,1,0:T(8,128)(2,1)} %bitcast.190), kind=kLoop, calls=%fused_computation.98 | loop fusion | bytes 4194304 | tf_op jit(solution)/shard_map/slice | solution.py:31
  150.3 3.3 %copy.103 = bf16[256,4096]{0,1:T(8,128)(2,1)S(1)} copy(bf16[256,4096]{1,0:T(8,128)(2,1)} %all-gather.3.cloned.1.call-done) | data formatting | bytes 4194304 | tf_op jit(solution)/shard_map/all_gather | solution.py:58
  163.8 1.4 fusion.86
  166.9 2.1 %copy.120 = f32[128,1024]{1,0:T(8,128)} copy(f32[128,1024]{0,1:T(8,128)} %bitcast.213) | data formatting | bytes 1048576 | tf_op jit(solution)/shard_map/reshape | solution.py:47
  172.2 2.0 %copy.119 = f32[128,1024]{1,0:T(8,128)} copy(f32[128,1024]{0,1:T(8,128)} %bitcast.214) | data formatting | bytes 1048576 | tf_op jit(solution)/shard_map/reshape | solution.py:47
  174.3 2.4 %fusion.9 = bf16[128,4096]{1,0:T(8,128)(2,1)} fusion(f32[128,1024]{1,0:T(8,128)S(1)} %copy.101, f32[128,1024]{1,0:T(8,128)S(1)} %copy.100, f32[128,1024]{1,0:T(8,128)S(1)} %copy-done, f32[128,1024]{1,0:T(8,128)S(1)} %copy-done.1, f32[128,1024]{1,0:T(8,128)S(1)} %copy.122, f32[128,1024]{1,0:T(8,128)S(1)} %copy.121, f32[128,1024]{1,0:T(8,128)} %copy.120, ...), kind=kLoop, calls=%fused_computation.22 | loop fusion | flops 4718592 | bytes 5259264 | tf_op jit(solution)/shard_map/convert_element_type | solution.py:80
  (87 shorter events, 29.7 us)
Async XLA Ops:
  6.5 8.0 %copy-start.10 = (bf16[128,4096]{1,0:T(8,128)(2,1)S(1)}, bf16[128,4096]{1,0:T(8,128)(2,1)}, u32[]{:S(2)}) copy-start(bf16[128,4096]{1,0:T(8,128)(2,1)} %param.9) | copy-start | bytes 3145732
  6.5 140.0 %all-gather.5.cloned.1.call-start = ((), (), s32[]{:S(2)}) async-start(), calls=%async_computation.1 | async-start | bytes 2228224 | tf_op jit(solution)/shard_map/all_gather | solution.py:59
  7.3 143.0 %all-gather.3.cloned.1.call-start = ((), (), s32[]{:S(2)}) async-start(), calls=%async_computation | async-start | bytes 2228224 | tf_op jit(solution)/shard_map/all_gather | solution.py:58
  8.9 56.2 %collective-permute-start = (bf16[128,4096]{0,1:T(8,128)(2,1)S(1)}, bf16[128,4096]{0,1:T(8,128)(2,1)}, u32[]{:S(2)}, u32[]{:S(2)}) collective-permute-start(bf16[128,4096]{0,1:T(8,128)(2,1)S(1)} %copy.76), channel_id=1, source_target_pairs={{0,1},{1,2},{2,3},{3,4},{4,5},{5,6},{6,7},{7,8},{8,9},{9,10},{10,1... | collective-permute-start | bytes 3145736 | tf_op jit(solution)/shard_map/ppermute | solution.py:15
  12.6 67.4 %collective-permute-start.2 = (bf16[128,4096]{0,1:T(8,128)(2,1)S(1)}, bf16[128,4096]{0,1:T(8,128)(2,1)}, u32[]{:S(2)}, u32[]{:S(2)}) collective-permute-start(bf16[128,4096]{0,1:T(8,128)(2,1)S(1)} %copy.76), channel_id=1, source_target_pairs={{1,0},{2,1},{3,2},{4,3},{5,4},{6,5},{7,6},{8,7},{9,8},{10,9},{11,1... | collective-permute-start | bytes 3145736 | tf_op jit(solution)/shard_map/ppermute | solution.py:15
  15.3 66.8 %collective-permute-start.4 = (bf16[128,4096]{0,1:T(8,128)(2,1)S(1)}, bf16[128,4096]{0,1:T(8,128)(2,1)}, u32[]{:S(2)}, u32[]{:S(2)}) collective-permute-start(bf16[128,4096]{0,1:T(8,128)(2,1)S(1)} %copy.79), channel_id=1, source_target_pairs={{0,1},{1,2},{2,3},{3,4},{4,5},{5,6},{6,7},{7,8},{8,9},{9,10},{10,1... | collective-permute-start | bytes 3145736 | tf_op jit(solution)/shard_map/ppermute | solution.py:15
  18.9 66.8 %collective-permute-start.6 = (bf16[128,4096]{0,1:T(8,128)(2,1)S(1)}, bf16[128,4096]{0,1:T(8,128)(2,1)}, u32[]{:S(2)}, u32[]{:S(2)}) collective-permute-start(bf16[128,4096]{0,1:T(8,128)(2,1)S(1)} %copy.79), channel_id=1, source_target_pairs={{1,0},{2,1},{3,2},{4,3},{5,4},{6,5},{7,6},{8,7},{9,8},{10,9},{11,1... | collective-permute-start | bytes 3145736 | tf_op jit(solution)/shard_map/ppermute | solution.py:15
  65.1 25.3 %collective-permute-start.1 = (bf16[128,4096]{0,1:T(8,128)(2,1)}, bf16[128,4096]{0,1:T(8,128)(2,1)}, u32[]{:S(2)}, u32[]{:S(2)}) collective-permute-start(bf16[128,4096]{0,1:T(8,128)(2,1)} %collective-permute-done), channel_id=1, source_target_pairs={{0,1},{1,2},{2,3},{3,4},{4,5},{5,6},{6,7},{7,8},{8,9},{9,10},{10,1... | collective-permute-start | bytes 3145736 | tf_op jit(solution)/shard_map/ppermute | solution.py:15
  80.1 46.4 %collective-permute-start.3 = (bf16[128,4096]{0,1:T(8,128)(2,1)}, bf16[128,4096]{0,1:T(8,128)(2,1)S(1)}, u32[]{:S(2)}, u32[]{:S(2)}) collective-permute-start(bf16[128,4096]{0,1:T(8,128)(2,1)} %collective-permute-done.2), channel_id=1, source_target_pairs={{1,0},{2,1},{3,2},{4,3},{5,4},{6,5},{7,6},{8,7},{9,8},{10,9},{11,1... | collective-permute-start | bytes 3145736 | tf_op jit(solution)/shard_map/ppermute | solution.py:15
  82.0 35.1 %collective-permute-start.5 = (bf16[128,4096]{0,1:T(8,128)(2,1)}, bf16[128,4096]{0,1:T(8,128)(2,1)S(1)}, u32[]{:S(2)}, u32[]{:S(2)}) collective-permute-start(bf16[128,4096]{0,1:T(8,128)(2,1)} %collective-permute-done.4), channel_id=1, source_target_pairs={{0,1},{1,2},{2,3},{3,4},{4,5},{5,6},{6,7},{7,8},{8,9},{9,10},{10,1... | collective-permute-start | bytes 3145736 | tf_op jit(solution)/shard_map/ppermute | solution.py:15
  85.7 38.8 %collective-permute-start.7 = (bf16[128,4096]{0,1:T(8,128)(2,1)}, bf16[128,4096]{0,1:T(8,128)(2,1)S(1)}, u32[]{:S(2)}, u32[]{:S(2)}) collective-permute-start(bf16[128,4096]{0,1:T(8,128)(2,1)} %collective-permute-done.6), channel_id=1, source_target_pairs={{1,0},{2,1},{3,2},{4,3},{5,4},{6,5},{7,6},{8,7},{9,8},{10,9},{11,1... | collective-permute-start | bytes 3145736 | tf_op jit(solution)/shard_map/ppermute | solution.py:15
  127.8 1.9 %copy-start.16 = (bf16[128,1024]{0,1:T(8,128)(2,1)S(1)}, bf16[128,1024]{0,1:T(8,128)(2,1)}, u32[]{:S(2)}) copy-start(bf16[128,1024]{0,1:T(8,128)(2,1)} %copy.159) | copy-start | bytes 786436
  129.7 1.0 copy-start.15
  153.5 1.2 copy-start.9
  154.8 1.0 copy-start.11
  155.6 2.7 %copy-start.7 = (bf16[1,256,1024]{2,1,0:T(8,128)(2,1)S(1)}, bf16[1,256,1024]{2,1,0:T(8,128)(2,1)}, u32[]{:S(2)}) copy-start(bf16[1,256,1024]{2,1,0:T(8,128)(2,1)} %get-tuple-element.31) | copy-start | bytes 1572868
  155.8 3.5 %copy-start.4 = (bf16[1,256,1024]{1,2,0:T(8,128)(2,1)S(1)}, bf16[1,256,1024]{1,2,0:T(8,128)(2,1)}, u32[]{:S(2)}) copy-start(bf16[1,256,1024]{1,2,0:T(8,128)(2,1)} %get-tuple-element.27) | copy-start | bytes 1572868
  155.8 3.5 %copy-start.8 = (bf16[128,1024]{0,1:T(8,128)(2,1)S(1)}, bf16[128,1024]{0,1:T(8,128)(2,1)}, u32[]{:S(2)}) copy-start(bf16[128,1024]{0,1:T(8,128)(2,1)} %copy.165) | copy-start | bytes 786436
  159.3 1.0 copy-start.13
  160.1 2.7 %copy-start.6 = (bf16[1,256,1024]{2,1,0:T(8,128)(2,1)S(1)}, bf16[1,256,1024]{2,1,0:T(8,128)(2,1)}, u32[]{:S(2)}) copy-start(bf16[1,256,1024]{2,1,0:T(8,128)(2,1)} %get-tuple-element.32) | copy-start | bytes 1572868
  160.3 3.5 %copy-start.3 = (bf16[1,256,1024]{1,2,0:T(8,128)(2,1)S(1)}, bf16[1,256,1024]{1,2,0:T(8,128)(2,1)}, u32[]{:S(2)}) copy-start(bf16[1,256,1024]{1,2,0:T(8,128)(2,1)} %get-tuple-element.28) | copy-start | bytes 1572868
  163.8 1.8 %copy-start.14 = (bf16[1,256,1024]{1,2,0:T(8,128)(2,1)S(1)}, bf16[1,256,1024]{1,2,0:T(8,128)(2,1)}, u32[]{:S(2)}) copy-start(bf16[1,256,1024]{1,2,0:T(8,128)(2,1)} %copy.110) | copy-start | bytes 1572868
  165.6 3.3 %copy-start.5 = (bf16[1,256,1024]{2,1,0:T(8,128)(2,1)S(1)}, bf16[1,256,1024]{2,1,0:T(8,128)(2,1)}, u32[]{:S(2)}) copy-start(bf16[1,256,1024]{2,1,0:T(8,128)(2,1)} %get-tuple-element.29) | copy-start | bytes 1572868
  165.7 4.3 %copy-start.2 = (bf16[1,256,1024]{1,2,0:T(8,128)(2,1)S(1)}, bf16[1,256,1024]{1,2,0:T(8,128)(2,1)}, u32[]{:S(2)}) copy-start(bf16[1,256,1024]{1,2,0:T(8,128)(2,1)} %get-tuple-element.25) | copy-start | bytes 1572868
  170.0 1.0 copy-start.12
  170.8 3.5 %copy-start = (f32[128,1024]{1,0:T(8,128)S(1)}, f32[128,1024]{1,0:T(8,128)}, u32[]{:S(2)}) copy-start(f32[128,1024]{1,0:T(8,128)} %copy.99) | copy-start | bytes 1572868
  170.8 3.5 %copy-start.1 = (f32[128,1024]{1,0:T(8,128)S(1)}, f32[128,1024]{1,0:T(8,128)}, u32[]{:S(2)}) copy-start(f32[128,1024]{1,0:T(8,128)} %copy.98) | copy-start | bytes 1572868
Sparse Core Ops, SparseCore 0:
  9.5 59.3 all-gather.4
  71.0 47.3 all-gather.2
where the time goes:
time: 185 us; the launch traced here: 184 us
  waiting for transfers between devices  76.1 us (41%)
  local copies, waits for them, and re-layouts  41.8 us (23%)
  starting transfers between devices  23.2 us (13%)
  matrix products  20.5 us (11%)
  between operations  14.5 us (8%)
  other arithmetic  7.45 us (4%)
    ppermute x8, waiting for transfers between devices, from_behind(): return lax.ppermute(block, axis, route)  75.4 us
    ppermute x8, starting transfers between devices, from_behind(): return lax.ppermute(block, axis, route)  23.2 us
    unnamed x52, local copies, waits for them, and re-layouts  15.7 us
    dot_general x8, matrix products, attend_blocks(): jnp.einsum('hqwk,wkhd->qhd', rounded, value_part, preferred_element_type=...  11.6 us
    reshape x8, local copies, waits for them, and re-layouts, attend_blocks(): pieces.append(result.reshape(row_count, head_group * head_dim))  8.94 us
    dot_general x8, matrix products, attend_blocks(): jnp.einsum('qhd,wkhd->hqwk', query_part, key_part, preferred_element_type...  8.9 us
    slice x6, local copies, waits for them, and re-layouts, attend_blocks(): value_stack[:, :, first:last]  8.67 us
    reduce_sum x5, other arithmetic, attend_blocks(): totals = jnp.sum(weights, axis=(2, 3))  4.15 us
  transfers between devices with their start and end apart: 10, of which 4 were waited for; matrix products, arithmetic and copies ran while one was open for 24% of the time, Pallas kernels for 0%

commit v1 on v0

v1 whole, which is shorter than its diff:
```python
import functools
import math

import jax
import jax.numpy as jnp
from jax import lax
from jax.experimental import pallas as pl
from jax.experimental.pallas import tpu as pltpu
from jax.sharding import PartitionSpec as P

HEADS = 32
RADIUS = 2
GROUPS = 8
AHEAD = 3
MESH = pl.DeviceIdType.MESH
OWN, PARTNER, NEAR, DIAG, FAR = range(5)


def softmax_parts(scores, scale):
    top = scores[0]
    for block in scores[1:]:
        top = jnp.maximum(top, block)
    top = jnp.max(top, axis=1, keepdims=True)
    weights = [jnp.exp2((block - top) * scale) for block in scores]
    total = weights[0]
    for block in weights[1:]:
        total = total + block
    total = jnp.sum(total, axis=1, keepdims=True)
    rounded = jnp.concatenate([block.astype(jnp.bfloat16) for block in weights], axis=1)
    return rounded, total


def scores_of(query, keys):
    return lax.dot_general(query, keys, (((1,), (1,)), ((), ())), preferred_element_type=jnp.float32)


def kernel(
    tiles, relay_text, step_ref, q_hbm, k_hbm, v_hbm, cq_hbm, tk_hbm, tv_hbm, gate_ref, out_ref,
    q_ref, cq_ref, kbuf, vbuf, tkbuf, tvbuf, self_acc, cross_acc,
    local_sem, own_sem, near_send, near_recv, relay_send, far_recv, part_send, part_recv, diag_send, diag_recv,
    half_send, half_recv, pair_send, pair_recv, share_send, share_recv, across_send,
):
    tokens, width = q_ref.shape
    head_dim = width // HEADS
    columns = width // GROUPS
    heads = HEADS // GROUPS
    depth = tiles // 4
    text_rows = tk_hbm.shape[0]

    t = lax.axis_index("tile")
    core = lax.rem(t, 2)
    side = lax.rem(t // 2, 2)
    place = t // 4
    partner = t + 1 - 2 * core
    buddy = t + 2 - 4 * side
    ahead = t + 4 - 8 * side
    behind = t - 4 + 8 * side
    has_ahead = (ahead >= 0) & (ahead < tiles)
    has_far = (behind >= 0) & (behind < tiles)
    has_up = place < depth - 1
    has_down = place > 0
    gives_near = side == core
    has_diag = has_far | (side != core)

    def remote(src, dst, send, recv, device):
        return pltpu.make_async_remote_copy(
            src_ref=src, dst_ref=dst, send_sem=send, recv_sem=recv, device_id={"tile": device}, device_id_type=MESH
        )

    def cols(g):
        return pl.ds(pl.multiple_of(g * columns, columns), columns)

    sources = (k_hbm, v_hbm)
    buffers = (kbuf, vbuf)
    texts = (tk_hbm, tv_hbm)
    text_buffers = (tkbuf, tvbuf)

    def local_copies():
        copies = [
            pltpu.make_async_copy(q_hbm, q_ref, local_sem.at[0]),
            pltpu.make_async_copy(cq_hbm, cq_ref, local_sem.at[1]),
        ]
        for i in range(2):
            copies.append(pltpu.make_async_copy(sources[i], buffers[i].at[OWN], own_sem.at[i]))
        if relay_text:
            row = ((place * 2 + core) * 2 + side) * text_rows
            for i in range(2):
                copies.append(
                    pltpu.make_async_copy(
                        texts[i],
                        text_buffers[i].at[pl.ds(pl.multiple_of(row, text_rows), text_rows), :],
                        local_sem.at[2 + i],
                    )
                )
        else:
            for i in range(2):
                copies.append(pltpu.make_async_copy(texts[i], text_buffers[i], local_sem.at[2 + i]))
        return copies

    for copy in local_copies():
        copy.start()

    barrier = pltpu.get_barrier_semaphore()

    def greet(device):
        pl.semaphore_signal(barrier, inc=1, device_id={"tile": device}, device_id_type=MESH)

    greet(partner)
    greet(buddy)

    @pl.when(has_up)
    def _():
        greet(t + 4)

    @pl.when(has_down)
    def _():
        greet(t - 4)

    pl.semaphore_wait(barrier, 2 + has_up.astype(jnp.int32) + has_down.astype(jnp.int32))

    def near_copy(g, i):
        return remote(
            sources[i].at[:, cols(g)], buffers[i].at[NEAR, :, cols(g)], near_send.at[g, i], near_recv.at[g, i], buddy
        )

    def part_copy(g, i):
        return remote(
            sources[i].at[:, cols(g)], buffers[i].at[PARTNER, :, cols(g)], part_send.at[g, i], part_recv.at[g, i], partner
        )

    def relay_copy(g, i):
        return remote(
            buffers[i].at[NEAR, :, cols(g)], buffers[i].at[FAR, :, cols(g)], relay_send.at[g, i], far_recv.at[g, i], ahead
        )

    def far_copy(g, i):
        return remote(
            buffers[i].at[NEAR, :, cols(g)], buffers[i].at[FAR, :, cols(g)], relay_send.at[g, i], far_recv.at[g, i], behind
        )

    def diag_copy(g, i, slot):
        return remote(
            buffers[i].at[slot, :, cols(g)], buffers[i].at[DIAG, :, cols(g)], diag_send.at[g, i], diag_recv.at[g, i], partner
        )

    def half_rows(which):
        row = ((place * 2 + core) * 2 + which) * text_rows
        return pl.ds(pl.multiple_of(row, text_rows), text_rows)

    def pair_rows(where, which):
        row = (where * 2 + which) * 2 * text_rows
        return pl.ds(pl.multiple_of(row, 2 * text_rows), 2 * text_rows)

    def half_copy(i, which):
        return remote(texts[i], text_buffers[i].at[half_rows(which), :], half_send.at[i], half_recv.at[i], buddy)

    def chain_copy(where, i, up):
        part = text_buffers[i].at[pair_rows(where, core), :]
        return remote(part, part, pair_send.at[where, i, int(up)], pair_recv.at[where, i], t + (4 if up else -4))

    def across_copy(where, i):
        part = text_buffers[i].at[pair_rows(where, core), :]
        return remote(part, part, across_send.at[where, i], pair_recv.at[where, i], buddy)

    def share_copy(where, i, which):
        part = text_buffers[i].at[pair_rows(where, which), :]
        return remote(part, part, share_send.at[where, i], share_recv.at[where, i], partner)

    def rides(i, up):
        return (side == (1 if up else 0)) if i == 1 else (side >= 0)

    def text_step(s):
        for up in (True, False):
            where = place - s if up else place + s
            inside = (where >= 0) if up else (where < depth)
            on = has_up if up else has_down
            for i in range(2):
                @pl.when(inside)
                def _():
                    chain_copy(where, i, up).wait_recv()

                    @pl.when(on & rides(i, up))
                    def _():
                        chain_copy(where, i, up).start()

                    if i == 1:
                        @pl.when(rides(i, up))
                        def _():
                            across_copy(where, i).start()

                    share_copy(where, i, core).start()

    def text_sends_done(s):
        for up in (True, False):
            where = place - s if up else place + s
            inside = (where >= 0) if up else (where < depth)
            on = has_up if up else has_down
            for i in range(2):
                @pl.when(inside)
                def _():
                    @pl.when(on & rides(i, up))
                    def _():
                        chain_copy(where, i, up).wait_send()

                    if i == 1:
                        @pl.when(rides(i, up))
                        def _():
                            across_copy(where, i).wait_send()

                    share_copy(where, i, core).wait_send()
                    share_copy(where, i, 1 - core).wait_recv()

    if relay_text:
        for i in range(2):
            half_copy(i, side).start()
    for g in range(min(AHEAD, GROUPS)):
        for i in range(2):
            near_copy(g, i).start()
            part_copy(g, i).start()
    for copy in local_copies():
        copy.wait()
    if relay_text:
        for i in range(2):
            half_copy(i, 1 - side).wait_recv()
            for up in (True, False):
                @pl.when((has_up if up else has_down) & rides(i, up))
                def _():
                    chain_copy(place, i, up).start()
            share_copy(place, i, core).start()

    scale = math.log2(math.e) / math.sqrt(head_dim)
    diag_slot = jnp.where(has_diag, DIAG, OWN)
    far_slot = jnp.where(has_far, FAR, OWN)

    def self_head(h):
        span = pl.ds(pl.multiple_of(h * head_dim, head_dim), head_dim)
        slots = (OWN, PARTNER, NEAR, diag_slot, far_slot)
        query = q_ref[:, span]
        keys = jnp.concatenate([kbuf[slot, :, span] for slot in slots], axis=0)
        values = jnp.concatenate([vbuf[slot, :, span] for slot in slots], axis=0)
        scores = scores_of(query, keys)
        blocks = [scores[:, n * tokens : (n + 1) * tokens] for n in range(5)]
        blocks[3] = jnp.where(has_diag, blocks[3], -1e30)
        blocks[4] = jnp.where(has_far, blocks[4], -1e30)
        rounded, total = softmax_parts(blocks, scale)
        summed = jnp.dot(rounded, values, preferred_element_type=jnp.float32)
        table = gate_ref[:, span].astype(jnp.float32)
        chosen = lax.broadcasted_iota(jnp.int32, table.shape, 0) == step_ref[0]
        gate = jnp.sum(jnp.where(chosen, table, 0.0), axis=0, keepdims=True)
        self_acc[:, span] = gate * (summed * (1.0 / total))

    def cross_head(h):
        span = pl.ds(pl.multiple_of(h * head_dim, head_dim), head_dim)
        scores = scores_of(cq_ref[:, span], tkbuf[:, span])
        pieces = scores.shape[1] // 128
        blocks = [scores[:, n * 128 : (n + 1) * 128] for n in range(pieces)]
        rounded, total = softmax_parts(blocks, scale)
        summed = jnp.dot(rounded, tvbuf[:, span], preferred_element_type=jnp.float32)
        cross_acc[:, span] = summed * (1.0 / total)

    text_rounds = 4
    steps_each = -(-(depth - 1) // text_rounds)
    cross_first = text_rounds + 1
    cross_rounds = GROUPS - cross_first
    cross_each = -(-HEADS // (2 * cross_rounds)) * 2

    def forward(g):
        for i in range(2):
            near_copy(g, i).wait_recv()

            @pl.when(has_ahead)
            def _():
                relay_copy(g, i).start()

            @pl.when(gives_near)
            def _():
                diag_copy(g, i, NEAR).start()

    def compute(g):
        for i in range(2):
            @pl.when(has_far)
            def _():
                far_copy(g, i).wait_recv()

                @pl.when(jnp.logical_not(gives_near))
                def _():
                    diag_copy(g, i, FAR).start()

        for i in range(2):
            part_copy(g, i).wait_recv()

            @pl.when(has_diag)
            def _():
                diag_copy(g, i, NEAR).wait_recv()

        def pair(n, carry):
            self_head(g * heads + 2 * n)
            self_head(g * heads + 2 * n + 1)
            return carry

        lax.fori_loop(0, heads // 2, pair, 0)

    def cross_round(r):
        @pl.when(r == cross_first)
        def _():
            if relay_text:
                for i in range(2):
                    share_copy(place, i, 1 - core).wait_recv()
                lax.fori_loop(1, depth, lambda s, c: (text_sends_done(s), c)[1], 0)

        def pair(n, carry):
            h = (r - cross_first) * cross_each + 2 * n

            @pl.when(h < HEADS)
            def _():
                cross_head(h)
                cross_head(h + 1)

            return carry

        lax.fori_loop(0, cross_each // 2, pair, 0)

    def round_of(r, carry):
        @pl.when(r < GROUPS)
        def _():
            forward(r)

        @pl.when(r + AHEAD < GROUPS)
        def _():
            for i in range(2):
                near_copy(r + AHEAD, i).start()
                part_copy(r + AHEAD, i).start()

        if relay_text:
            @pl.when((r >= 1) & (r <= text_rounds))
            def _():
                def one(j, c):
                    s = (r - 1) * steps_each + j + 1

                    @pl.when(s < depth)
                    def _():
                        text_step(s)

                    return c

                lax.fori_loop(0, steps_each, one, 0)

        @pl.when((r >= cross_first) & (r < GROUPS))
        def _():
            cross_round(r)

        @pl.when(r >= 1)
        def _():
            compute(r - 1)

        return carry

    lax.fori_loop(0, GROUPS + 1, round_of, 0)

    def finish(g, carry):
        out_ref[:, cols(g)] = (self_acc[:, cols(g)] + cross_acc[:, cols(g)]).astype(out_ref.dtype)
        for i in range(2):
            near_copy(g, i).wait_send()
            part_copy(g, i).wait_send()

            @pl.when(has_ahead)
            def _():
                relay_copy(g, i).wait_send()

            @pl.when(gives_near | has_far)
            def _():
                diag_copy(g, i, NEAR).wait_send()

        return carry

    lax.fori_loop(0, GROUPS, finish, 0)
    if relay_text:
        for i in range(2):
            half_copy(i, side).wait_send()
            for up in (True, False):
                @pl.when((has_up if up else has_down) & rides(i, up))
                def _():
                    chain_copy(place, i, up).wait_send()
            share_copy(place, i, core).wait_send()


def shards(self_query, self_key, self_value, cross_query, text_key, text_value, timestep, gate_table):
    tiles = lax.axis_size("tile")
    depth = tiles // 4
    tokens, width = self_query.shape
    text_total = text_key.shape[0] * tiles
    relay_text = text_key.shape[0] % 16 == 0
    if not relay_text:
        text_key = lax.all_gather(text_key, "tile", axis=0, tiled=True)
        text_value = lax.all_gather(text_value, "tile", axis=0, tiled=True)
    anywhere = pl.BlockSpec(memory_space=pl.ANY)
    vmem = pl.BlockSpec(memory_space=pltpu.VMEM)
    smem = pl.BlockSpec(memory_space=pltpu.SMEM)
    dma = pltpu.SemaphoreType.DMA
    bf16, f32 = jnp.bfloat16, jnp.float32
    return pl.pallas_call(
        functools.partial(kernel, tiles, relay_text),
        out_shape=jax.ShapeDtypeStruct((tokens, width), bf16),
        in_specs=[smem] + [anywhere] * 6 + [vmem],
        out_specs=vmem,
        scratch_shapes=[
            pltpu.VMEM((tokens, width), bf16),
            pltpu.VMEM((tokens, width), bf16),
            pltpu.VMEM((5, tokens, width), bf16),
            pltpu.VMEM((5, tokens, width), bf16),
            pltpu.VMEM((text_total, width), bf16),
            pltpu.VMEM((text_total, width), bf16),
            pltpu.VMEM((tokens, width), f32),
            pltpu.VMEM((tokens, width), f32),
            dma((4,)),
            dma((2,)),
        ]
        + [dma((GROUPS, 2))] * 8
        + [dma((2,)), dma((2,)), dma((depth, 2, 2)), dma((depth, 2)), dma((depth, 2)), dma((depth, 2)), dma((depth, 2))],
        compiler_params=pltpu.CompilerParams(
            collective_id=0, has_side_effects=True, vmem_limit_bytes=40 * 1024 * 1024
        ),
    )(timestep, self_query, self_key, self_value, cross_query, text_key, text_value, gate_table)


def solution(mesh):
    rows = P(("groups", "tile"), None)
    return jax.shard_map(
        shards, mesh=mesh, in_specs=(rows,) * 6 + (P(), P()), out_specs=rows, check_vma=False
    )
```

time: 185 us -> 113 us (0.61)
  the two profiles are of different devices: /device:TPU:17 before, /device:TPU:24 now
where the time goes in v1:
time: 113 us; the launch traced here: 112 us
  Pallas kernels  103 us (91%)
  local copies, waits for them, and re-layouts  8.69 us (8%)
    pallas_call x1, Pallas kernels, shards(): pl.pallas_call(functools.partial(kernel, tiles, relay_text), out_shape=ja...  103 us
    unnamed x15, local copies, waits for them, and re-layouts  8.69 us

profile of v1, /device:TPU:24, one launch (start us, length us, event | category | flops | bytes accessed | tf_op | source)
XLA Modules:
  0.0 112.4 jit_solution(14330204917598355029)
XLA Ops:
  0.7 0.0 copy-start
  0.7 1.2 %copy-done = bf16[128,4096]{1,0:T(8,128)(2,1)S(1)} copy-done((bf16[128,4096]{1,0:T(8,128)(2,1)S(1)}, bf16[128,4096]{1,0:T(8,128)(2,1)}, u32[]{:S(2)}) %copy-start) | copy-done | bytes 1048600
  1.9 0.0 copy-start.1
  1.9 1.2 %copy-done.1 = bf16[128,4096]{1,0:T(8,128)(2,1)S(1)} copy-done((bf16[128,4096]{1,0:T(8,128)(2,1)S(1)}, bf16[128,4096]{1,0:T(8,128)(2,1)}, u32[]{:S(2)}) %copy-start.1) | copy-done | bytes 1048600
  3.1 0.0 copy-start.2
  3.1 1.2 %copy-done.2 = bf16[128,4096]{1,0:T(8,128)(2,1)S(1)} copy-done((bf16[128,4096]{1,0:T(8,128)(2,1)S(1)}, bf16[128,4096]{1,0:T(8,128)(2,1)}, u32[]{:S(2)}) %copy-start.2) | copy-done | bytes 1048600
  4.3 0.0 copy-start.3
  4.3 1.2 %copy-done.3 = bf16[128,4096]{1,0:T(8,128)(2,1)S(1)} copy-done((bf16[128,4096]{1,0:T(8,128)(2,1)S(1)}, bf16[128,4096]{1,0:T(8,128)(2,1)}, u32[]{:S(2)}) %copy-start.3) | copy-done | bytes 1048600
  5.6 0.0 copy-start.4
  5.6 1.0 copy-done.4
  6.6 0.0 copy-start.5
  6.6 0.9 copy-done.5
  7.5 0.0 copy-start.6
  7.5 0.9 copy-done.6
  8.4 103.0 %shard_map.82 = bf16[128,4096]{1,0:T(8,128)(2,1)S(1)} custom-call(s32[1]{0:T(128)S(6)} %copy.10.step_ref, bf16[128,4096]{1,0:T(8,128)(2,1)S(1)} %copy-done, bf16[128,4096]{1,0:T(8,128)(2,1)S(1)} %copy-done.1, bf16[128,4096]{1,0:T(8,128)(2,1)S(1)} %copy-done.2, bf16[128,4096]{1,0:T(8,128)(2,1)S(1)} %copy-done.3, bf16[16,4096]{1,0:T(8,128)(2,1)S(1)} %copy-done.5, ...), custom_call_target="tpu_custom_call" | custom-call | tf_op jit(solution)/shard_map/pallas_call | solution.py:401
  111.4 1.0 copy.11
Async XLA Ops:
  0.7 1.2 %copy-start = (bf16[128,4096]{1,0:T(8,128)(2,1)S(1)}, bf16[128,4096]{1,0:T(8,128)(2,1)}, u32[]{:S(2)}) copy-start(bf16[128,4096]{1,0:T(8,128)(2,1)} %q_hbm.1) | copy-start | bytes 3145732
  1.9 1.2 %copy-start.1 = (bf16[128,4096]{1,0:T(8,128)(2,1)S(1)}, bf16[128,4096]{1,0:T(8,128)(2,1)}, u32[]{:S(2)}) copy-start(bf16[128,4096]{1,0:T(8,128)(2,1)} %k_hbm.1) | copy-start | bytes 3145732
  3.1 1.2 %copy-start.2 = (bf16[128,4096]{1,0:T(8,128)(2,1)S(1)}, bf16[128,4096]{1,0:T(8,128)(2,1)}, u32[]{:S(2)}) copy-start(bf16[128,4096]{1,0:T(8,128)(2,1)} %v_hbm.1) | copy-start | bytes 3145732
  4.3 1.2 %copy-start.3 = (bf16[128,4096]{1,0:T(8,128)(2,1)S(1)}, bf16[128,4096]{1,0:T(8,128)(2,1)}, u32[]{:S(2)}) copy-start(bf16[128,4096]{1,0:T(8,128)(2,1)} %cq_hbm.1) | copy-start | bytes 3145732
  5.6 1.0 copy-start.4
  6.6 0.9 copy-start.5
  7.5 0.9 copy-start.6

commit v2 on v1

--- a/solution.py
+++ b/solution.py
@@ -11,7 +11,9 @@
 HEADS = 32
 RADIUS = 2
 GROUPS = 8
-AHEAD = 3
+AHEAD = 8
+LAG = 2
+TEXT_GAP = 1
 MESH = pl.DeviceIdType.MESH
 OWN, PARTNER, NEAR, DIAG, FAR = range(5)
 
@@ -35,8 +37,8 @@
 
 
 def kernel(
-    tiles, relay_text, step_ref, q_hbm, k_hbm, v_hbm, cq_hbm, tk_hbm, tv_hbm, gate_ref, out_ref,
-    q_ref, cq_ref, kbuf, vbuf, tkbuf, tvbuf, self_acc, cross_acc,
+    tiles, relay_text, step_ref, q_hbm, k_hbm, v_hbm, cq_hbm, tk_hbm, tv_hbm, gate_hbm, out_ref,
+    q_ref, cq_ref, gate_ref, kbuf, vbuf, tkbuf, tvbuf, self_acc, cross_acc,
     local_sem, own_sem, near_send, near_recv, relay_send, far_recv, part_send, part_recv, diag_send, diag_recv,
     half_send, half_recv, pair_send, pair_recv, share_send, share_recv, across_send,
 ):
@@ -79,6 +81,7 @@
         copies = [
             pltpu.make_async_copy(q_hbm, q_ref, local_sem.at[0]),
             pltpu.make_async_copy(cq_hbm, cq_ref, local_sem.at[1]),
+            pltpu.make_async_copy(gate_hbm, gate_ref, local_sem.at[4]),
         ]
         for i in range(2):
             copies.append(pltpu.make_async_copy(sources[i], buffers[i].at[OWN], own_sem.at[i]))
@@ -175,20 +178,27 @@
             inside = (where >= 0) if up else (where < depth)
             on = has_up if up else has_down
             for i in range(2):
-                @pl.when(inside)
+                @pl.when(inside & rides(i, up))
                 def _():
                     chain_copy(where, i, up).wait_recv()
 
-                    @pl.when(on & rides(i, up))
+                    @pl.when(on)
                     def _():
                         chain_copy(where, i, up).start()
 
                     if i == 1:
-                        @pl.when(rides(i, up))
-                        def _():
-                            across_copy(where, i).start()
-
+                        across_copy(where, i).start()
                     share_copy(where, i, core).start()
+
+    def across_step(s):
+        for up in (True, False):
+            where = place - s if up else place + s
+            inside = (where >= 0) if up else (where < depth)
+
+            @pl.when(inside & jnp.logical_not(rides(1, up)))
+            def _():
+                across_copy(where, 1).wait_recv()
+                share_copy(where, 1, core).start()
 
     def text_sends_done(s):
         for up in (True, False):
@@ -258,12 +268,6 @@
         summed = jnp.dot(rounded, tvbuf[:, span], preferred_element_type=jnp.float32)
         cross_acc[:, span] = summed * (1.0 / total)
 
-    text_rounds = 4
-    steps_each = -(-(depth - 1) // text_rounds)
-    cross_first = text_rounds + 1
-    cross_rounds = GROUPS - cross_first
-    cross_each = -(-HEADS // (2 * cross_rounds)) * 2
-
     def forward(g):
         for i in range(2):
             near_copy(g, i).wait_recv()
@@ -293,32 +297,8 @@
             def _():
                 diag_copy(g, i, NEAR).wait_recv()
 
-        def pair(n, carry):
-            self_head(g * heads + 2 * n)
-            self_head(g * heads + 2 * n + 1)
-            return carry
-
-        lax.fori_loop(0, heads // 2, pair, 0)
-
-    def cross_round(r):
-        @pl.when(r == cross_first)
-        def _():
-            if relay_text:
-                for i in range(2):
-                    share_copy(place, i, 1 - core).wait_recv()
-                lax.fori_loop(1, depth, lambda s, c: (text_sends_done(s), c)[1], 0)
-
-        def pair(n, carry):
-            h = (r - cross_first) * cross_each + 2 * n
-
-            @pl.when(h < HEADS)
-            def _():
-                cross_head(h)
-                cross_head(h + 1)
-
-            return carry
-
-        lax.fori_loop(0, cross_each // 2, pair, 0)
+        for n in range(heads):
+            self_head(g * heads + n)
 
     def round_of(r, carry):
         @pl.when(r < GROUPS)
@@ -332,30 +312,35 @@
                 part_copy(r + AHEAD, i).start()
 
         if relay_text:
-            @pl.when((r >= 1) & (r <= text_rounds))
-            def _():
-                def one(j, c):
-                    s = (r - 1) * steps_each + j + 1
-
-                    @pl.when(s < depth)
-                    def _():
-                        text_step(s)
-
-                    return c
-
-                lax.fori_loop(0, steps_each, one, 0)
-
-        @pl.when((r >= cross_first) & (r < GROUPS))
+            def one(s, c):
+                @pl.when(r == jnp.minimum(s * TEXT_GAP - 1, GROUPS - 1))
+                def _():
+                    text_step(s)
+
+                return c
+
+            lax.fori_loop(1, depth, one, 0)
+
+        @pl.when(r >= LAG)
         def _():
-            cross_round(r)
-
-        @pl.when(r >= 1)
-        def _():
-            compute(r - 1)
+            compute(r - LAG)
 
         return carry
 
-    lax.fori_loop(0, GROUPS + 1, round_of, 0)
+    lax.fori_loop(0, GROUPS + LAG, round_of, 0)
+
+    if relay_text:
+        lax.fori_loop(1, depth, lambda s, c: (across_step(s), c)[1], 0)
+        for i in range(2):
+            share_copy(place, i, 1 - core).wait_recv()
+        lax.fori_loop(1, depth, lambda s, c: (text_sends_done(s), c)[1], 0)
+
+    def cross_pair(n, carry):
+        for j in range(4):
+            cross_head(4 * n + j)
+        return carry
+
+    lax.fori_loop(0, HEADS // 4, cross_pair, 0)
 
     def finish(g, carry):
         out_ref[:, cols(g)] = (self_acc[:, cols(g)] + cross_acc[:, cols(g)]).astype(out_ref.dtype)
@@ -401,24 +386,25 @@
     return pl.pallas_call(
         functools.partial(kernel, tiles, relay_text),
         out_shape=jax.ShapeDtypeStruct((tokens, width), bf16),
-        in_specs=[smem] + [anywhere] * 6 + [vmem],
+        in_specs=[smem] + [anywhere] * 7,
         out_specs=vmem,
         scratch_shapes=[
             pltpu.VMEM((tokens, width), bf16),
             pltpu.VMEM((tokens, width), bf16),
+            pltpu.VMEM(gate_table.shape, bf16),
             pltpu.VMEM((5, tokens, width), bf16),
             pltpu.VMEM((5, tokens, width), bf16),
             pltpu.VMEM((text_total, width), bf16),
             pltpu.VMEM((text_total, width), bf16),
             pltpu.VMEM((tokens, width), f32),
             pltpu.VMEM((tokens, width), f32),
-            dma((4,)),
+            dma((5,)),
             dma((2,)),
         ]
         + [dma((GROUPS, 2))] * 8
         + [dma((2,)), dma((2,)), dma((depth, 2, 2)), dma((depth, 2)), dma((depth, 2)), dma((depth, 2)), dma((depth, 2))],
         compiler_params=pltpu.CompilerParams(
-            collective_id=0, has_side_effects=True, vmem_limit_bytes=40 * 1024 * 1024
+            collective_id=0, has_side_effects=True, vmem_limit_bytes=60 * 1024 * 1024
         ),
     )(timestep, self_query, self_key, self_value, cross_query, text_key, text_value, gate_table)
 

time: 113 us -> 86.7 us (0.77)
  the two profiles are of different devices: /device:TPU:24 before, /device:TPU:7 now
where the time goes in v2:
time: 86.7 us; the launch traced here: 86.6 us
  Pallas kernels  83.6 us (96%)
  local copies, waits for them, and re-layouts  2.29 us (3%)
    pallas_call x1, Pallas kernels, shards(): pl.pallas_call(functools.partial(kernel, tiles, relay_text), out_shape=ja...  83.6 us
    unnamed x1, local copies, waits for them, and re-layouts  2.29 us

profile of v2, /device:TPU:7, one launch (start us, length us, event | category | flops | bytes accessed | tf_op | source)
XLA Modules:
  0.0 86.6 jit_solution(7638413440663372044)
XLA Ops:
  0.7 83.6 %shard_map.82 = bf16[128,4096]{1,0:T(8,128)(2,1)} custom-call(s32[1]{0:T(128)S(6)} %copy.10.step_ref, bf16[128,4096]{1,0:T(8,128)(2,1)} %q_hbm.1, bf16[128,4096]{1,0:T(8,128)(2,1)} %k_hbm.1, bf16[128,4096]{1,0:T(8,128)(2,1)} %v_hbm.1, bf16[128,4096]{1,0:T(8,128)(2,1)} %cq_hbm.1, bf16[16,4096]{1,0:T(8,128)(2,1)} %tk_hbm.1, bf16[16,4096]{1,0:T(8,128)(2,1)} %tv_hbm.1, ...), custom_call_target="tpu_custom_call" | custom-call | tf_op jit(solution)/shard_map/pallas_call | solution.py:386
  84.3 2.3 %copy.11 = bf16[128,4096]{1,0:T(8,128)(2,1)} copy(bf16[128,4096]{1,0:T(8,128)(2,1)} %shard_map.82) | data formatting | bytes 2097152

commit v3 on v2

--- a/solution.py
+++ b/solution.py
@@ -12,8 +12,11 @@
 RADIUS = 2
 GROUPS = 8
 AHEAD = 8
-LAG = 2
+LAG = 3
 TEXT_GAP = 1
+SCORE_ROUND = 7
+EARLY_HEADS = 32
+UNROLL = 4
 MESH = pl.DeviceIdType.MESH
 OWN, PARTNER, NEAR, DIAG, FAR = range(5)
 
@@ -38,7 +41,7 @@
 
 def kernel(
     tiles, relay_text, step_ref, q_hbm, k_hbm, v_hbm, cq_hbm, tk_hbm, tv_hbm, gate_hbm, out_ref,
-    q_ref, cq_ref, gate_ref, kbuf, vbuf, tkbuf, tvbuf, self_acc, cross_acc,
+    q_ref, cq_ref, gate_ref, kbuf, vbuf, tkbuf, tvbuf, self_acc, cross_acc, weight_ref,
     local_sem, own_sem, near_send, near_recv, relay_send, far_recv, part_send, part_recv, diag_send, diag_recv,
     half_send, half_recv, pair_send, pair_recv, share_send, share_recv, across_send,
 ):
@@ -146,6 +149,16 @@
             buffers[i].at[slot, :, cols(g)], buffers[i].at[DIAG, :, cols(g)], diag_send.at[g, i], diag_recv.at[g, i], partner
         )
 
+    early = EARLY_HEADS * head_dim
+    pieces = ((0, 0, early, False), (1, 0, width, True))
+    if early < width:
+        pieces += ((0, early, width - early, True),)
+    late = range(1, len(pieces))
+
+    def text_part(n, rows):
+        i, first, count, _ = pieces[n]
+        return text_buffers[i].at[rows, pl.ds(first, count)]
+
     def half_rows(which):
         row = ((place * 2 + core) * 2 + which) * text_rows
         return pl.ds(pl.multiple_of(row, text_rows), text_rows)
@@ -158,26 +171,26 @@
         return remote(texts[i], text_buffers[i].at[half_rows(which), :], half_send.at[i], half_recv.at[i], buddy)
 
     def chain_copy(where, i, up):
-        part = text_buffers[i].at[pair_rows(where, core), :]
+        part = text_part(i, pair_rows(where, core))
         return remote(part, part, pair_send.at[where, i, int(up)], pair_recv.at[where, i], t + (4 if up else -4))
 
     def across_copy(where, i):
-        part = text_buffers[i].at[pair_rows(where, core), :]
+        part = text_part(i, pair_rows(where, core))
         return remote(part, part, across_send.at[where, i], pair_recv.at[where, i], buddy)
 
     def share_copy(where, i, which):
-        part = text_buffers[i].at[pair_rows(where, which), :]
+        part = text_part(i, pair_rows(where, which))
         return remote(part, part, share_send.at[where, i], share_recv.at[where, i], partner)
 
     def rides(i, up):
-        return (side == (1 if up else 0)) if i == 1 else (side >= 0)
+        return (side == (1 if up else 0)) if pieces[i][3] else (side >= 0)
 
     def text_step(s):
         for up in (True, False):
             where = place - s if up else place + s
             inside = (where >= 0) if up else (where < depth)
             on = has_up if up else has_down
-            for i in range(2):
+            for i in range(len(pieces)):
                 @pl.when(inside & rides(i, up))
                 def _():
                     chain_copy(where, i, up).wait_recv()
@@ -186,7 +199,7 @@
                     def _():
                         chain_copy(where, i, up).start()
 
-                    if i == 1:
+                    if pieces[i][3]:
                         across_copy(where, i).start()
                     share_copy(where, i, core).start()
 
@@ -197,28 +210,43 @@
 
             @pl.when(inside & jnp.logical_not(rides(1, up)))
             def _():
-                across_copy(where, 1).wait_recv()
-                share_copy(where, 1, core).start()
+                for i in late:
+                    across_copy(where, i).wait_recv()
+                    share_copy(where, i, core).start()
 
     def text_sends_done(s):
         for up in (True, False):
             where = place - s if up else place + s
             inside = (where >= 0) if up else (where < depth)
             on = has_up if up else has_down
-            for i in range(2):
+            for i in range(len(pieces)):
                 @pl.when(inside)
                 def _():
                     @pl.when(on & rides(i, up))
                     def _():
                         chain_copy(where, i, up).wait_send()
 
-                    if i == 1:
+                    if pieces[i][3]:
                         @pl.when(rides(i, up))
                         def _():
                             across_copy(where, i).wait_send()
 
                     share_copy(where, i, core).wait_send()
+
+    def shared(s, arrays):
+        for up in (True, False):
+            where = place - s if up else place + s
+            inside = (where >= 0) if up else (where < depth)
+
+            @pl.when(inside)
+            def _():
+                for i in arrays:
                     share_copy(where, i, 1 - core).wait_recv()
+
+    def all_shared(arrays):
+        for i in arrays:
+            share_copy(place, i, 1 - core).wait_recv()
+        lax.fori_loop(1, depth, lambda s, c: (shared(s, arrays), c)[1], 0)
 
     if relay_text:
         for i in range(2):
@@ -232,6 +260,7 @@
     if relay_text:
         for i in range(2):
             half_copy(i, 1 - side).wait_recv()
+        for i in range(len(pieces)):
             for up in (True, False):
                 @pl.when((has_up if up else has_down) & rides(i, up))
                 def _():
@@ -259,14 +288,18 @@
         gate = jnp.sum(jnp.where(chosen, table, 0.0), axis=0, keepdims=True)
         self_acc[:, span] = gate * (summed * (1.0 / total))
 
-    def cross_head(h):
+    def cross_scores(h):
         span = pl.ds(pl.multiple_of(h * head_dim, head_dim), head_dim)
         scores = scores_of(cq_ref[:, span], tkbuf[:, span])
-        pieces = scores.shape[1] // 128
-        blocks = [scores[:, n * 128 : (n + 1) * 128] for n in range(pieces)]
+        blocks = [scores[:, n * 128 : (n + 1) * 128] for n in range(scores.shape[1] // 128)]
         rounded, total = softmax_parts(blocks, scale)
-        summed = jnp.dot(rounded, tvbuf[:, span], preferred_element_type=jnp.float32)
-        cross_acc[:, span] = summed * (1.0 / total)
+        weight_ref[h] = rounded
+        cross_acc[:, span] = jnp.broadcast_to(1.0 / total, (tokens, head_dim))
+
+    def cross_values(h):
+        span = pl.ds(pl.multiple_of(h * head_dim, head_dim), head_dim)
+        summed = jnp.dot(weight_ref[h], tvbuf[:, span], preferred_element_type=jnp.float32)
+        out_ref[:, span] = (self_acc[:, span] + summed * cross_acc[:, span]).astype(out_ref.dtype)
 
     def forward(g):
         for i in range(2):
@@ -325,25 +358,46 @@
         def _():
             compute(r - LAG)
 
+        @pl.when(r >= SCORE_ROUND)
+        def _():
+            if relay_text:
+                @pl.when(r == SCORE_ROUND)
+                def _():
+                    all_shared((0,))
+
+            def four(n, c):
+                for j in range(UNROLL):
+                    cross_scores((r - SCORE_ROUND) * score_heads + UNROLL * n + j)
+                return c
+
+            lax.fori_loop(0, score_heads // UNROLL, four, 0)
+
         return carry
 
+    score_heads = EARLY_HEADS // (GROUPS + LAG - SCORE_ROUND)
     lax.fori_loop(0, GROUPS + LAG, round_of, 0)
 
     if relay_text:
         lax.fori_loop(1, depth, lambda s, c: (across_step(s), c)[1], 0)
-        for i in range(2):
-            share_copy(place, i, 1 - core).wait_recv()
+        all_shared(late)
+
+    def late_scores(n, carry):
+        for j in range(4):
+            cross_scores(EARLY_HEADS + 4 * n + j)
+        return carry
+
+    lax.fori_loop(0, (HEADS - EARLY_HEADS) // 4, late_scores, 0)
+
+    def cross_four(n, carry):
+        for j in range(8):
+            cross_values(8 * n + j)
+        return carry
+
+    lax.fori_loop(0, HEADS // 8, cross_four, 0)
+    if relay_text:
         lax.fori_loop(1, depth, lambda s, c: (text_sends_done(s), c)[1], 0)
 
-    def cross_pair(n, carry):
-        for j in range(4):
-            cross_head(4 * n + j)
-        return carry
-
-    lax.fori_loop(0, HEADS // 4, cross_pair, 0)
-
     def finish(g, carry):
-        out_ref[:, cols(g)] = (self_acc[:, cols(g)] + cross_acc[:, cols(g)]).astype(out_ref.dtype)
         for i in range(2):
             near_copy(g, i).wait_send()
             part_copy(g, i).wait_send()
@@ -362,6 +416,7 @@
     if relay_text:
         for i in range(2):
             half_copy(i, side).wait_send()
+        for i in range(len(pieces)):
             for up in (True, False):
                 @pl.when((has_up if up else has_down) & rides(i, up))
                 def _():
@@ -398,11 +453,12 @@
             pltpu.VMEM((text_total, width), bf16),
             pltpu.VMEM((tokens, width), f32),
             pltpu.VMEM((tokens, width), f32),
+            pltpu.VMEM((HEADS, tokens, text_total), bf16),
             dma((5,)),
             dma((2,)),
         ]
         + [dma((GROUPS, 2))] * 8
-        + [dma((2,)), dma((2,)), dma((depth, 2, 2)), dma((depth, 2)), dma((depth, 2)), dma((depth, 2)), dma((depth, 2))],
+        + [dma((2,)), dma((2,)), dma((depth, 3, 2))] + [dma((depth, 3))] * 4,
         compiler_params=pltpu.CompilerParams(
             collective_id=0, has_side_effects=True, vmem_limit_bytes=60 * 1024 * 1024
         ),

time: 86.7 us -> 84.6 us (0.976)
  Pallas kernels: 83.6 us -> 80.9 us
    pallas_call x1, Pallas kernels: 83.6 us -> 80.9 us  [shards(): pl.pallas_call(functools.partial(kernel, tiles, relay_text), out_shape=ja...]
where the time goes in v3:
time: 84.6 us; the launch traced here: 83.8 us
  Pallas kernels  80.9 us (96%)
  local copies, waits for them, and re-layouts  2.29 us (3%)
    pallas_call x1, Pallas kernels, shards(): pl.pallas_call(functools.partial(kernel, tiles, relay_text), out_shape=ja...  80.9 us
    unnamed x1, local copies, waits for them, and re-layouts  2.29 us

profile of v3, /device:TPU:7, one launch (start us, length us, event | category | flops | bytes accessed | tf_op | source)
XLA Modules:
  0.0 83.8 jit_solution(15539908448983538881)
XLA Ops:
  0.7 80.9 %shard_map.82 = bf16[128,4096]{1,0:T(8,128)(2,1)} custom-call(s32[1]{0:T(128)S(6)} %copy.10.step_ref, bf16[128,4096]{1,0:T(8,128)(2,1)} %q_hbm.1, bf16[128,4096]{1,0:T(8,128)(2,1)} %k_hbm.1, bf16[128,4096]{1,0:T(8,128)(2,1)} %v_hbm.1, bf16[128,4096]{1,0:T(8,128)(2,1)} %cq_hbm.1, bf16[16,4096]{1,0:T(8,128)(2,1)} %tk_hbm.1, bf16[16,4096]{1,0:T(8,128)(2,1)} %tv_hbm.1, ...), custom_call_target="tpu_custom_call" | custom-call | tf_op jit(solution)/shard_map/pallas_call | solution.py:441
  81.5 2.3 %copy.11 = bf16[128,4096]{1,0:T(8,128)(2,1)} copy(bf16[128,4096]{1,0:T(8,128)(2,1)} %shard_map.82) | data formatting | bytes 2097152
